TPU v7x, 32 devices: a whole 2x2x4 slice. The times are simulated.
32 devices in a mesh: dom: 8 (over z, y), ray: 4 (over x, core).
Axes of the slice: x: 2, y: 2, z: 4, core: 2. Of those that a mesh axis runs over, the one named last changes fastest.
Arguments:
- projections: bfloat16 [8, 64, 8192], P('dom', None, 'ray'), may hold values from -6 to 6
- phase_kernel: bfloat16 [129], replicated, may hold values from -0.5 to 0.5
- image: bfloat16 [16384, 64], P('dom'), may hold values from -6 to 6
- tile_library: bfloat16 [8, 4, 16, 128, 128], P('dom', 'ray'), may hold values from -0.09375 to 0.09375
- tile_entry: int32 [8, 4, 256], P('dom', 'ray'), may hold values from 0 to 15
- tile_image: int32 [8, 4, 256], P('dom', 'ray'), may hold values from 0 to 15
- tile_slot: int32 [8, 4, 256], P('dom', 'ray'), may hold values from 0 to 7
- tile_count: int32 [8, 4], P('dom', 'ray'), may hold values from 64 to 256, as said below
- slot_block: int32 [8, 4, 8], P('dom', 'ray'), may hold values from 0 to 15
Outputs:
- residual: bfloat16 [8, 64, 8192], P('dom', None, 'ray')
- image_next: float32 [16384, 64], P(('dom', 'ray'))
Inputs may be any that keep to these rules, and one draw needn't show every extreme that they name: `tile_count`: each device has at most 256 live tiles; some device holds exactly 256. Entries beyond a device's count are not used.
All inputs are finite; a program needn't handle non-finite values.
Results may differ from a plain program's by a relative error of at most 0.0075.
Values may be sent and summed in bfloat16 or wider, within the bound.
A program may use at most 64 MiB of HBM per device.

v0:
```python
import jax
import jax.numpy as jnp
from jax import lax
from jax.sharding import PartitionSpec as P

SMOOTH = 8
relax_factor = 0.25


def with_halo(cells, sides, width):
    for axis, dim in sides:
        count = lax.axis_size(axis)
        ends = count - 1
        head = lax.slice_in_dim(cells, 0, width, axis=dim)
        tail = lax.slice_in_dim(cells, cells.shape[dim] - width, cells.shape[dim], axis=dim)
        cells = jnp.concatenate(
            [
                lax.ppermute(tail, axis, [(i, (i + 1) % count) for i in range(ends)]),
                cells,
                lax.ppermute(head, axis, [((i + 1) % count, i) for i in range(ends)]),
            ],
            axis=dim,
        )
    return cells


def toeplitz(kernel, tile_size):
    taps = kernel.shape[0]
    padded = jnp.concatenate([kernel, jnp.zeros((2 * tile_size + 1 - taps,), kernel.dtype)])
    tiled = jnp.tile(padded, tile_size)[: 2 * tile_size * tile_size]
    return tiled.reshape(tile_size, 2 * tile_size).T


def phase_filter(projections, phase_kernel, tile_size):
    half_width = (phase_kernel.shape[0] - 1) // 2
    angles, slices, columns = projections.shape
    block_count = columns // tile_size
    rimmed = with_halo(projections, (("ray", 2),), half_width)
    padded = jnp.pad(rimmed, ((0, 0), (0, 0), (0, 2 * tile_size - 2 * half_width)))
    blocks = padded.reshape(angles, slices, block_count + 2, tile_size)
    windows = jnp.concatenate(
        [blocks[:, :, :block_count], blocks[:, :, 1 : block_count + 1]], axis=-1
    )
    filtered = jnp.einsum(
        "asbi,ij->asbj",
        windows,
        toeplitz(phase_kernel, tile_size),
        preferred_element_type=jnp.float32,
    )
    return filtered.reshape(angles, slices, columns).astype(jnp.bfloat16)


def stripe_profile(gathered):
    profile = jnp.median(gathered.astype(jnp.float32), axis=0)
    columns = profile.shape[1]
    rimmed = with_halo(profile, (("ray", 1),), SMOOTH)
    window_sum = jnp.zeros_like(profile)
    for offset in range(2 * SMOOTH + 1):
        window_sum = window_sum + rimmed[:, offset : offset + columns]
    position = lax.axis_index("ray") * columns + jnp.arange(columns)
    detector = lax.axis_size("ray") * columns
    in_range = (
        jnp.minimum(position + SMOOTH, detector - 1) - jnp.maximum(position - SMOOTH, 0) + 1
    ).astype(jnp.float32)
    return (profile - window_sum / in_range).astype(jnp.bfloat16)


def shards(
    projections,
    phase_kernel,
    image,
    tile_library,
    tile_entry,
    tile_image,
    tile_slot,
    tile_count,
    slot_block,
):
    tile_size = tile_library.shape[-1]
    angles, slices, columns = projections.shape
    phase = phase_filter(projections, phase_kernel, tile_size)
    gathered = lax.all_to_all(phase, "dom", split_axis=1, concat_axis=0, tiled=True)
    stripe = stripe_profile(gathered)
    fixed_rows = (gathered.astype(jnp.float32) - stripe.astype(jnp.float32)[None]).astype(
        jnp.bfloat16
    )
    corrected = lax.all_to_all(fixed_rows, "dom", split_axis=0, concat_axis=1, tiled=True)
    owners = lax.axis_size("dom")
    library = tile_library[0, 0]
    entries = tile_entry[0, 0]
    images = tile_image[0, 0]
    slots = tile_slot[0, 0]
    capacity = entries.shape[0]
    block_size = 64
    turn_count = capacity // block_size
    image_blocks = image.reshape(-1, tile_size, slices)
    block_total = image_blocks.shape[0]
    live_mask = jnp.arange(capacity) < tile_count[0, 0]
    slot_target = jnp.where(live_mask, slots, owners)
    image_target = jnp.where(live_mask, images, block_total)

    def forward_turn(turn_index, partial_value):
        first_tile = turn_index * block_size
        chosen = lax.dynamic_slice_in_dim(entries, first_tile, block_size)
        placed = lax.dynamic_slice_in_dim(images, first_tile, block_size)
        destined = lax.dynamic_slice_in_dim(slot_target, first_tile, block_size)
        product = jnp.einsum(
            "krp,kps->ksr",
            library[chosen],
            image_blocks[placed],
            preferred_element_type=jnp.float32,
        )
        return partial_value.at[destined].add(product, mode="drop")

    partial_value = lax.fori_loop(
        0, turn_count, forward_turn, jnp.zeros((owners, slices, tile_size), jnp.float32)
    )
    received = lax.all_to_all(
        partial_value.astype(jnp.bfloat16), "dom", split_axis=0, concat_axis=0, tiled=True
    )
    per_owner = columns // tile_size
    carried = slot_block[0, 0]
    block_ids = jnp.arange(angles * per_owner).reshape(angles, per_owner)
    selector = (block_ids[:, :, None] == carried[None, None, :]).astype(jnp.bfloat16)
    forward = jnp.einsum("abd,dst->asbt", selector, received, preferred_element_type=jnp.float32)
    residual = (corrected.astype(jnp.float32) - forward.reshape(angles, slices, columns)).astype(
        jnp.bfloat16
    )
    back = jnp.einsum(
        "abd,asbt->dst",
        selector,
        residual.reshape(angles, slices, per_owner, tile_size),
        preferred_element_type=jnp.float32,
    ).astype(jnp.bfloat16)
    returned = lax.all_to_all(back, "dom", split_axis=0, concat_axis=0, tiled=True)

    def adjoint_turn(turn_index, gradient):
        first_tile = turn_index * block_size
        chosen = lax.dynamic_slice_in_dim(entries, first_tile, block_size)
        sourced = lax.dynamic_slice_in_dim(slots, first_tile, block_size)
        destined = lax.dynamic_slice_in_dim(image_target, first_tile, block_size)
        product = jnp.einsum(
            "krp,ksr->kps", library[chosen], returned[sourced], preferred_element_type=jnp.float32
        )
        return gradient.at[destined].add(product, mode="drop")

    gradient = lax.fori_loop(
        0, turn_count, adjoint_turn, jnp.zeros((block_total, tile_size, slices), jnp.float32)
    )
    gradient = gradient.reshape(-1, slices)
    rows_own = gradient.shape[0] // lax.axis_size("ray")
    update = lax.psum_scatter(gradient, "ray", scatter_dimension=0, tiled=True)
    own_image = lax.dynamic_slice_in_dim(image, lax.axis_index("ray") * rows_own, rows_own)
    image_next = own_image.astype(jnp.float32) + relax_factor * update
    return (residual, image_next)


def solution(mesh):
    return jax.shard_map(
        shards,
        mesh=mesh,
        in_specs=(
            P("dom", None, "ray"),
            P(),
            P("dom", None),
            P("dom", "ray", None, None, None),
            P("dom", "ray", None),
            P("dom", "ray", None),
            P("dom", "ray", None),
            P("dom", "ray"),
            P("dom", "ray", None),
        ),
        out_specs=(P("dom", None, "ray"), P(("dom", "ray"), None)),
        check_vma=False,
    )
```

profile of v0, /device:TPU:0, one launch (start us, length us, event | category | flops | bytes accessed | tf_op | source)
XLA Modules:
  0.0 196.1 jit_solution(8649035580683881368)
XLA Ops:
  8.0 2.4 %collective-permute-start = (bf16[1,64,64]{2,1,0:T(8,128)(2,1)S(1)}, bf16[1,64,64]{2,1,0:T(8,128)(2,1)S(1)}, u32[]{:S(2)}, u32[]{:S(2)}) collective-permute-start(bf16[1,64,64]{2,1,0:T(8,128)(2,1)S(1)} %get-tuple-element.333), channel_id=1, source_target_pairs={{0,1},{1,2},{2,3},{4,5},{5,6},{6,7},{8,9},{9,10},{10,11},{12,13},{... | collective-permute-start | bytes 24584 | tf_op jit(solution)/shard_map/ppermute | solution.py:18
  21.2 6.4 %all-to-all-start = ((bf16[8,2,8192]{2,1,0:T(2,128)(2,1)}), bf16[8,2,8192]{2,1,0:T(2,128)(2,1)}, u32[]{:S(2)}, u32[]{:S(2)}) async-start(bf16[8,2,8192]{2,1,0:T(2,128)(2,1)} %reshape.296), calls=%async_computation | async-start | bytes 524288 | tf_op jit(solution)/shard_map/all_to_all | solution.py:82
  27.7 47.9 %while.28 = (s32[]{:T(128)}, f32[8,64,128]{2,1,0:T(8,128)S(1)}, s32[256]{0:T(256)S(1)}, s32[256]{0:T(256)S(1)}, bf16[16,128,64]{2,1,0:T(8,128)(2,1)S(1)}, /*inde...) while((s32[]{:T(128)}, f32[8,64,128]{2,1,0:T(8,128)S(1)}, ...), condition=%wide.region_4.5_spmd, body=%wide.region_2.4_spmd.sunk | while | flops 134744640 | bytes 17836972 | solution.py:115
  27.9 2.2 %gather_fusion = bf16[64,128,64]{2,1,0:T(8,128)(2,1)} fusion(bf16[16,128,64]{2,1,0:T(8,128)(2,1)S(1)} %get-tuple-element.456, s32[1024]{0:T(1024)S(1)} %pad_clamp_fusion.8), kind=kCustom, calls=%fused_computation.clone.1 | custom fusion | bytes 2097408 | tf_op jit(solution)/shard_map/while/body/eval_jaxpr/gather | solution.py:110
  32.2 3.7 %fusion.71 = f32[64,64,128]{2,1,0:T(8,128)S(1)} fusion(bf16[64,128,64]{2,1,0:T(8,128)(2,1)} %gather_fusion, bf16[64,128,128]{2,1,0:T(8,128)(2,1)} %gather_fusion.1), kind=kOutput, calls=%fused_computation.113.clone.1 | convolution fusion | flops 134217728 | bytes 5242880 | tf_op jit(solution)/shard_map/while/body/eval_jaxpr/krp,kps->ksr/dot_general | solution.py:107
  35.9 3.8 %scatter_fusion = f32[8,64,128]{2,1,0:T(8,128)S(1)} fusion(f32[8,64,128]{2,1,0:T(8,128)S(1)} %get-tuple-element.442, s32[64]{0:T(128)S(1)} %compare_select_fusion.10, f32[64,64,128]{2,1,0:T(8,128)S(1)} %fusion.71), kind=kCustom, calls=%fused_computation.4.clone.1 | custom fusion | flops 524288 | bytes 6291712 | tf_op jit(solution)/shard_map/while/body/eval_jaxpr/scatter-add | solution.py:113
  39.9 2.2 %gather_fusion = bf16[64,128,64]{2,1,0:T(8,128)(2,1)} fusion(bf16[16,128,64]{2,1,0:T(8,128)(2,1)S(1)} %get-tuple-element.456, s32[1024]{0:T(1024)S(1)} %pad_clamp_fusion.8), kind=kCustom, calls=%fused_computation.clone.1 | custom fusion | bytes 2097408 | tf_op jit(solution)/shard_map/while/body/eval_jaxpr/gather | solution.py:110
  44.1 3.7 %fusion.71 = f32[64,64,128]{2,1,0:T(8,128)S(1)} fusion(bf16[64,128,64]{2,1,0:T(8,128)(2,1)} %gather_fusion, bf16[64,128,128]{2,1,0:T(8,128)(2,1)} %gather_fusion.1), kind=kOutput, calls=%fused_computation.113.clone.1 | convolution fusion | flops 134217728 | bytes 5242880 | tf_op jit(solution)/shard_map/while/body/eval_jaxpr/krp,kps->ksr/dot_general | solution.py:107
  47.9 3.8 %scatter_fusion = f32[8,64,128]{2,1,0:T(8,128)S(1)} fusion(f32[8,64,128]{2,1,0:T(8,128)S(1)} %get-tuple-element.442, s32[64]{0:T(128)S(1)} %compare_select_fusion.10, f32[64,64,128]{2,1,0:T(8,128)S(1)} %fusion.71), kind=kCustom, calls=%fused_computation.4.clone.1 | custom fusion | flops 524288 | bytes 6291712 | tf_op jit(solution)/shard_map/while/body/eval_jaxpr/scatter-add | solution.py:113
  51.8 2.2 %gather_fusion = bf16[64,128,64]{2,1,0:T(8,128)(2,1)} fusion(bf16[16,128,64]{2,1,0:T(8,128)(2,1)S(1)} %get-tuple-element.456, s32[1024]{0:T(1024)S(1)} %pad_clamp_fusion.8), kind=kCustom, calls=%fused_computation.clone.1 | custom fusion | bytes 2097408 | tf_op jit(solution)/shard_map/while/body/eval_jaxpr/gather | solution.py:110
  56.1 3.7 %fusion.71 = f32[64,64,128]{2,1,0:T(8,128)S(1)} fusion(bf16[64,128,64]{2,1,0:T(8,128)(2,1)} %gather_fusion, bf16[64,128,128]{2,1,0:T(8,128)(2,1)} %gather_fusion.1), kind=kOutput, calls=%fused_computation.113.clone.1 | convolution fusion | flops 134217728 | bytes 5242880 | tf_op jit(solution)/shard_map/while/body/eval_jaxpr/krp,kps->ksr/dot_general | solution.py:107
  59.9 3.8 %scatter_fusion = f32[8,64,128]{2,1,0:T(8,128)S(1)} fusion(f32[8,64,128]{2,1,0:T(8,128)S(1)} %get-tuple-element.442, s32[64]{0:T(128)S(1)} %compare_select_fusion.10, f32[64,64,128]{2,1,0:T(8,128)S(1)} %fusion.71), kind=kCustom, calls=%fused_computation.4.clone.1 | custom fusion | flops 524288 | bytes 6291712 | tf_op jit(solution)/shard_map/while/body/eval_jaxpr/scatter-add | solution.py:113
  63.8 2.2 %gather_fusion = bf16[64,128,64]{2,1,0:T(8,128)(2,1)} fusion(bf16[16,128,64]{2,1,0:T(8,128)(2,1)S(1)} %get-tuple-element.456, s32[1024]{0:T(1024)S(1)} %pad_clamp_fusion.8), kind=kCustom, calls=%fused_computation.clone.1 | custom fusion | bytes 2097408 | tf_op jit(solution)/shard_map/while/body/eval_jaxpr/gather | solution.py:110
  68.1 3.7 %fusion.71 = f32[64,64,128]{2,1,0:T(8,128)S(1)} fusion(bf16[64,128,64]{2,1,0:T(8,128)(2,1)} %gather_fusion, bf16[64,128,128]{2,1,0:T(8,128)(2,1)} %gather_fusion.1), kind=kOutput, calls=%fused_computation.113.clone.1 | convolution fusion | flops 134217728 | bytes 5242880 | tf_op jit(solution)/shard_map/while/body/eval_jaxpr/krp,kps->ksr/dot_general | solution.py:107
  71.8 3.8 %scatter_fusion = f32[8,64,128]{2,1,0:T(8,128)S(1)} fusion(f32[8,64,128]{2,1,0:T(8,128)S(1)} %get-tuple-element.442, s32[64]{0:T(128)S(1)} %compare_select_fusion.10, f32[64,64,128]{2,1,0:T(8,128)S(1)} %fusion.71), kind=kCustom, calls=%fused_computation.4.clone.1 | custom fusion | flops 524288 | bytes 6291712 | tf_op jit(solution)/shard_map/while/body/eval_jaxpr/scatter-add | solution.py:113
  76.3 6.0 %all-to-all-start.2 = ((bf16[8,64,128]{2,1,0:T(8,128)(2,1)}), bf16[8,64,128]{2,1,0:T(8,128)(2,1)S(1)}, u32[]{:S(2)}, u32[]{:S(2)}) async-start(bf16[8,64,128]{2,1,0:T(8,128)(2,1)} %convert_element_type.108), calls=%async_computation.2 | async-start | bytes 262144 | tf_op jit(solution)/shard_map/all_to_all | solution.py:118
  84.2 4.8 %sort.16 = (f32[8,8,2048]{2,0,1:T(8,128)S(1)}, s32[8,8,2048]{2,0,1:T(8,128)}) sort(f32[8,8,2048]{2,0,1:T(8,128)S(1)} %copy_select_fusion, s32[8,8,2048]{2,0,1:T(8,128)S(1)} %iota.19), dimensions={0}, to_apply=%region_1.2 | sort | flops 2228224 | bytes 2097152 | tf_op jit(solution)/shard_map/jit(median)/jit(quantile)/sort | solution.py:54
  90.5 4.1 %collective-permute-start.2 = (f32[8,8]{1,0:T(8,128)S(1)}, f32[8,8]{1,0:T(8,128)S(1)}, u32[]{:S(2)}, u32[]{:S(2)}) collective-permute-start(f32[8,8]{1,0:T(8,128)S(1)} %get-tuple-element.334), channel_id=1, source_target_pairs={{0,1},{1,2},{2,3},{4,5},{5,6},{6,7},{8,9},{9,10},{10,11},{12,13},{... | collective-permute-start | bytes 776 | tf_op jit(solution)/shard_map/ppermute | solution.py:18
  96.6 5.7 %all-to-all-start.1 = ((bf16[8,8,2048]{2,1,0:T(8,128)(2,1)}), bf16[8,8,2048]{2,1,0:T(8,128)(2,1)S(1)}, u32[]{:S(2)}, u32[]{:S(2)}) async-start(bf16[8,8,2048]{2,1,0:T(8,128)(2,1)} %subtract_convert_fusion), calls=%async_computation.1 | async-start | bytes 524288 | tf_op jit(solution)/shard_map/all_to_all | solution.py:87
  102.7 8.1 %all-to-all-done.1 = bf16[8,8,2048]{2,1,0:T(8,128)(2,1)S(1)} async-done(((bf16[8,8,2048]{2,1,0:T(8,128)(2,1)}), bf16[8,8,2048]{2,1,0:T(8,128)(2,1)S(1)}, u32[]{:S(2)}, u32[]{:S(2)}) %all-to-all-start.1) | async-done | bytes 262176 | tf_op jit(solution)/shard_map/all_to_all | solution.py:87
  111.8 5.0 %all-to-all-start.3 = ((bf16[8,64,128]{2,1,0:T(8,128)(2,1)}), bf16[8,64,128]{2,1,0:T(8,128)(2,1)S(1)}, u32[]{:S(2)}, u32[]{:S(2)}) async-start(bf16[8,64,128]{2,1,0:T(8,128)(2,1)} %copy.34), calls=%async_computation.3 | async-start | bytes 262144 | tf_op jit(solution)/shard_map/all_to_all | solution.py:135
  116.9 7.4 %all-to-all-done.3 = bf16[8,64,128]{2,1,0:T(8,128)(2,1)S(1)} async-done(((bf16[8,64,128]{2,1,0:T(8,128)(2,1)}), bf16[8,64,128]{2,1,0:T(8,128)(2,1)S(1)}, u32[]{:S(2)}, u32[]{:S(2)}) %all-to-all-start.3) | async-done | bytes 131104 | tf_op jit(solution)/shard_map/all_to_all | solution.py:135
  124.3 41.5 %while.29 = (s32[]{:T(128)}, f32[16,128,64]{1,2,0:T(8,128)S(1)}, s32[256]{0:T(256)S(1)}, s32[256]{0:T(256)S(1)}, bf16[16,128,128]{2,1,0:T(8,128)(2,1)S(1)}, /*in...) while((s32[]{:T(128)}, f32[16,128,64]{1,2,0:T(8,128)S(1)}, ...), condition=%wide.region_7.8_spmd, body=%wide.region_5.7_spmd.sunk | while | flops 134744640 | bytes 17836972 | solution.py:147
  128.4 2.6 %fusion.74 = f32[64,128,64]{1,2,0:T(8,128)S(1)} fusion(bf16[64,64,128]{2,1,0:T(8,128)(2,1)} %gather_fusion.2, bf16[64,128,128]{2,1,0:T(8,128)(2,1)} %gather_fusion.3), kind=kOutput, calls=%fused_computation.114.clone.1 | convolution fusion | flops 134217728 | bytes 5242880 | tf_op jit(solution)/shard_map/while/body/eval_jaxpr/krp,ksr->kps/dot_general | solution.py:142
  131.0 3.7 %scatter_fusion.1 = f32[16,128,64]{1,2,0:T(8,128)S(1)} fusion(f32[16,128,64]{1,2,0:T(8,128)S(1)} %get-tuple-element.475, s32[64]{0:T(128)S(1)} %compare_select_fusion.12, f32[64,128,64]{1,2,0:T(8,128)S(1)} %fusion.74), kind=kCustom, calls=%fused_computation.5.clone.1 | custom fusion | flops 524288 | bytes 6291712 | tf_op jit(solution)/shard_map/while/body/eval_jaxpr/scatter-add | solution.py:145
  138.7 2.6 %fusion.74 = f32[64,128,64]{1,2,0:T(8,128)S(1)} fusion(bf16[64,64,128]{2,1,0:T(8,128)(2,1)} %gather_fusion.2, bf16[64,128,128]{2,1,0:T(8,128)(2,1)} %gather_fusion.3), kind=kOutput, calls=%fused_computation.114.clone.1 | convolution fusion | flops 134217728 | bytes 5242880 | tf_op jit(solution)/shard_map/while/body/eval_jaxpr/krp,ksr->kps/dot_general | solution.py:142
  141.3 3.8 %scatter_fusion.1 = f32[16,128,64]{1,2,0:T(8,128)S(1)} fusion(f32[16,128,64]{1,2,0:T(8,128)S(1)} %get-tuple-element.475, s32[64]{0:T(128)S(1)} %compare_select_fusion.12, f32[64,128,64]{1,2,0:T(8,128)S(1)} %fusion.74), kind=kCustom, calls=%fused_computation.5.clone.1 | custom fusion | flops 524288 | bytes 6291712 | tf_op jit(solution)/shard_map/while/body/eval_jaxpr/scatter-add | solution.py:145
  149.1 2.6 %fusion.74 = f32[64,128,64]{1,2,0:T(8,128)S(1)} fusion(bf16[64,64,128]{2,1,0:T(8,128)(2,1)} %gather_fusion.2, bf16[64,128,128]{2,1,0:T(8,128)(2,1)} %gather_fusion.3), kind=kOutput, calls=%fused_computation.114.clone.1 | convolution fusion | flops 134217728 | bytes 5242880 | tf_op jit(solution)/shard_map/while/body/eval_jaxpr/krp,ksr->kps/dot_general | solution.py:142
  151.7 3.8 %scatter_fusion.1 = f32[16,128,64]{1,2,0:T(8,128)S(1)} fusion(f32[16,128,64]{1,2,0:T(8,128)S(1)} %get-tuple-element.475, s32[64]{0:T(128)S(1)} %compare_select_fusion.12, f32[64,128,64]{1,2,0:T(8,128)S(1)} %fusion.74), kind=kCustom, calls=%fused_computation.5.clone.1 | custom fusion | flops 524288 | bytes 6291712 | tf_op jit(solution)/shard_map/while/body/eval_jaxpr/scatter-add | solution.py:145
  159.5 2.6 %fusion.74 = f32[64,128,64]{1,2,0:T(8,128)S(1)} fusion(bf16[64,64,128]{2,1,0:T(8,128)(2,1)} %gather_fusion.2, bf16[64,128,128]{2,1,0:T(8,128)(2,1)} %gather_fusion.3), kind=kOutput, calls=%fused_computation.114.clone.1 | convolution fusion | flops 134217728 | bytes 5242880 | tf_op jit(solution)/shard_map/while/body/eval_jaxpr/krp,ksr->kps/dot_general | solution.py:142
  162.1 3.8 %scatter_fusion.1 = f32[16,128,64]{1,2,0:T(8,128)S(1)} fusion(f32[16,128,64]{1,2,0:T(8,128)S(1)} %get-tuple-element.475, s32[64]{0:T(128)S(1)} %compare_select_fusion.12, f32[64,128,64]{1,2,0:T(8,128)S(1)} %fusion.74), kind=kCustom, calls=%fused_computation.5.clone.1 | custom fusion | flops 524288 | bytes 6291712 | tf_op jit(solution)/shard_map/while/body/eval_jaxpr/scatter-add | solution.py:145
  168.6 19.1 %reduce-scatter.2.cloned.1.call-done = f32[512,64]{0,1:T(8,128)} async-done(((f32[2048,64]{0,1:T(8,128)}), f32[512,64]{0,1:T(8,128)}) %reduce-scatter.2.cloned.1.call-update) | async-done | bytes 131088 | tf_op jit(solution)/shard_map/reduce_scatter | solution.py:152
  (107 shorter events, 47.8 us)
Async XLA Ops:
  8.0 7.3 %collective-permute-start = (bf16[1,64,64]{2,1,0:T(8,128)(2,1)S(1)}, bf16[1,64,64]{2,1,0:T(8,128)(2,1)S(1)}, u32[]{:S(2)}, u32[]{:S(2)}) collective-permute-start(bf16[1,64,64]{2,1,0:T(8,128)(2,1)S(1)} %get-tuple-element.333), channel_id=1, source_target_pairs={{0,1},{1,2},{2,3},{4,5},{5,6},{6,7},{8,9},{9,10},{10,11},{12,13},{... | collective-permute-start | bytes 24584 | tf_op jit(solution)/shard_map/ppermute | solution.py:18
  10.4 5.2 %collective-permute-start.1 = (bf16[1,64,64]{2,1,0:T(8,128)(2,1)S(1)}, bf16[1,64,64]{2,1,0:T(8,128)(2,1)S(1)}, u32[]{:S(2)}, u32[]{:S(2)}) collective-permute-start(bf16[1,64,64]{2,1,0:T(8,128)(2,1)S(1)} %get-tuple-element.332), channel_id=1, source_target_pairs={{1,0},{2,1},{3,2},{5,4},{6,5},{7,6},{9,8},{10,9},{11,10},{13,12},{... | collective-permute-start | bytes 24584 | tf_op jit(solution)/shard_map/ppermute | solution.py:20
  17.1 10.6 %copy-start = (bf16[1,1,16,128,128]{4,3,2,1,0:T(8,128)(2,1)S(1)}, bf16[1,1,16,128,128]{4,3,2,1,0:T(8,128)(2,1)}, u32[]{:S(2)}) copy-start(bf16[1,1,16,128,128]{4,3,2,1,0:T(8,128)(2,1)} %param.16) | copy-start | bytes 1572868
  17.1 10.6 %copy-start.2 = (s32[1,1,256]{2,1,0:T(1,128)S(1)}, s32[1,1,256]{2,1,0:T(1,128)}, u32[]{:S(2)}) copy-start(s32[1,1,256]{2,1,0:T(1,128)} %param.17) | copy-start | bytes 3076
  17.1 10.6 %copy-start.3 = (s32[1,1,256]{2,1,0:T(1,128)S(1)}, s32[1,1,256]{2,1,0:T(1,128)}, u32[]{:S(2)}) copy-start(s32[1,1,256]{2,1,0:T(1,128)} %param.18) | copy-start | bytes 3076
  21.2 55.1 %all-to-all-start = ((bf16[8,2,8192]{2,1,0:T(2,128)(2,1)}), bf16[8,2,8192]{2,1,0:T(2,128)(2,1)}, u32[]{:S(2)}, u32[]{:S(2)}) async-start(bf16[8,2,8192]{2,1,0:T(2,128)(2,1)} %reshape.296), calls=%async_computation | async-start | bytes 524288 | tf_op jit(solution)/shard_map/all_to_all | solution.py:82
  76.3 20.3 %all-to-all-start.2 = ((bf16[8,64,128]{2,1,0:T(8,128)(2,1)}), bf16[8,64,128]{2,1,0:T(8,128)(2,1)S(1)}, u32[]{:S(2)}, u32[]{:S(2)}) async-start(bf16[8,64,128]{2,1,0:T(8,128)(2,1)} %convert_element_type.108), calls=%async_computation.2 | async-start | bytes 262144 | tf_op jit(solution)/shard_map/all_to_all | solution.py:118
  83.8 18.5 %copy-start.5 = (s32[1,1,8]{2,1,0:T(1,128)S(1)}, s32[1,1,8]{2,1,0:T(1,128)}, u32[]{:S(2)}) copy-start(s32[1,1,8]{2,1,0:T(1,128)} %param.21) | copy-start | bytes 100
  89.2 5.4 %collective-permute-start.3 = (f32[8,8]{1,0:T(8,128)S(1)}, f32[8,8]{1,0:T(8,128)S(1)}, u32[]{:S(2)}, u32[]{:S(2)}) collective-permute-start(f32[8,8]{1,0:T(8,128)S(1)} %get-tuple-element.335), channel_id=1, source_target_pairs={{1,0},{2,1},{3,2},{5,4},{6,5},{7,6},{9,8},{10,9},{11,10},{13,12},{... | collective-permute-start | bytes 776 | tf_op jit(solution)/shard_map/ppermute | solution.py:20
  90.5 4.9 %collective-permute-start.2 = (f32[8,8]{1,0:T(8,128)S(1)}, f32[8,8]{1,0:T(8,128)S(1)}, u32[]{:S(2)}, u32[]{:S(2)}) collective-permute-start(f32[8,8]{1,0:T(8,128)S(1)} %get-tuple-element.334), channel_id=1, source_target_pairs={{0,1},{1,2},{2,3},{4,5},{5,6},{6,7},{8,9},{9,10},{10,11},{12,13},{... | collective-permute-start | bytes 776 | tf_op jit(solution)/shard_map/ppermute | solution.py:18
  96.6 14.2 %all-to-all-start.1 = ((bf16[8,8,2048]{2,1,0:T(8,128)(2,1)}), bf16[8,8,2048]{2,1,0:T(8,128)(2,1)S(1)}, u32[]{:S(2)}, u32[]{:S(2)}) async-start(bf16[8,8,2048]{2,1,0:T(8,128)(2,1)} %subtract_convert_fusion), calls=%async_computation.1 | async-start | bytes 524288 | tf_op jit(solution)/shard_map/all_to_all | solution.py:87
  102.7 9.2 %copy-start.1 = (f32[1,64,16,128]{3,2,1,0:T(8,128)}, f32[1,64,16,128]{3,2,1,0:T(8,128)S(1)}, u32[]{:S(2)}) copy-start(f32[1,64,16,128]{3,2,1,0:T(8,128)S(1)} %convolution_bitcast_fusion) | copy-start | bytes 1572868
  102.7 21.7 %copy-start.4 = (s32[1,1,256]{2,1,0:T(1,128)S(1)}, s32[1,1,256]{2,1,0:T(1,128)}, u32[]{:S(2)}) copy-start(s32[1,1,256]{2,1,0:T(1,128)} %param.19) | copy-start | bytes 3076
  111.8 12.5 %all-to-all-start.3 = ((bf16[8,64,128]{2,1,0:T(8,128)(2,1)}), bf16[8,64,128]{2,1,0:T(8,128)(2,1)S(1)}, u32[]{:S(2)}, u32[]{:S(2)}) async-start(bf16[8,64,128]{2,1,0:T(8,128)(2,1)} %copy.34), calls=%async_computation.3 | async-start | bytes 262144 | tf_op jit(solution)/shard_map/all_to_all | solution.py:135
  116.8 70.9 %reduce-scatter.2.cloned.1.call-start = ((), (), s32[]{:S(2)}) async-start(), calls=%async_computation.5 | async-start | bytes 655360 | tf_op jit(solution)/shard_map/reduce_scatter | solution.py:152
Sparse Core Ops, SparseCore 0:
  166.8 20.8 reduce-scatter.1
where the time goes:
time: 197 us; the launch traced here: 196 us
  other arithmetic  44 us (22%)
  local copies, waits for them, and re-layouts  42.8 us (22%)
  waiting for transfers between devices  35.6 us (18%)
  starting transfers between devices  32.2 us (16%)
  matrix products  26.2 us (13%)
  between operations  15 us (8%)
    reduce_scatter x1, waiting for transfers between devices, shards(): update = lax.psum_scatter(gradient, 'ray', scatter_dimension=0, tiled=True)  19.1 us
    scatter-add x4, other arithmetic, forward_turn(): return partial_value.at[destined].add(product, mode='drop')  15 us
    scatter-add x4, other arithmetic, adjoint_turn(): return gradient.at[destined].add(product, mode='drop')  15 us
    dot_general x4, matrix products, forward_turn(): jnp.einsum('krp,kps->ksr', library[chosen], image_blocks[placed], preferr...  15 us
    dot_general x4, matrix products, adjoint_turn(): jnp.einsum('krp,ksr->kps', library[chosen], returned[sourced], preferred_...  10.4 us
    gather x4, local copies, waits for them, and re-layouts, forward_turn(): image_blocks[placed]  8.67 us
    gather x4, local copies, waits for them, and re-layouts, adjoint_turn(): library[chosen]  8.66 us
    gather x4, local copies, waits for them, and re-layouts, forward_turn(): library[chosen]  8.43 us
  transfers between devices with their start and end apart: 9, of which 5 were waited for; matrix products, arithmetic and copies ran while one was open for 31% of the time, Pallas kernels for 0%

commit v1 on v0

--- a/solution.py
+++ b/solution.py
@@ -84,7 +84,10 @@
     fixed_rows = (gathered.astype(jnp.float32) - stripe.astype(jnp.float32)[None]).astype(
         jnp.bfloat16
     )
-    corrected = lax.all_to_all(fixed_rows, "dom", split_axis=0, concat_axis=1, tiled=True)
+    corrected = jnp.concatenate(
+        lax.all_to_all(jnp.stack(jnp.split(fixed_rows, lax.axis_size("dom"), axis=0)), "dom", 0, 0),
+        axis=1,
+    )
     owners = lax.axis_size("dom")
     library = tile_library[0, 0]
     entries = tile_entry[0, 0]

time: 197 us -> 201 us (1.020)
  local copies, waits for them, and re-layouts: 42.8 us -> 47.7 us
    unnamed x18 -> x25, local copies, waits for them, and re-layouts: 4.05 us -> 8.37 us
  transfers between devices with their start and end apart: 9 -> 9, of which waited for: 5 -> 5; matrix products, arithmetic and copies ran while one was open for 31% -> 33% of each run, Pallas kernels for 0% -> 0%
where the time goes in v1:
time: 201 us; the launch traced here: 200 us
  local copies, waits for them, and re-layouts  47.7 us (24%)
  other arithmetic  43.3 us (22%)
  waiting for transfers between devices  35.6 us (18%)
  starting transfers between devices  32.2 us (16%)
  matrix products  26.2 us (13%)
  between operations  15 us (7%)
    reduce_scatter x1, waiting for transfers between devices, shards(): update = lax.psum_scatter(gradient, 'ray', scatter_dimension=0, tiled=True)  19.1 us
    scatter-add x4, other arithmetic, forward_turn(): return partial_value.at[destined].add(product, mode='drop')  15 us
    scatter-add x4, other arithmetic, adjoint_turn(): return gradient.at[destined].add(product, mode='drop')  15 us
    dot_general x4, matrix products, forward_turn(): jnp.einsum('krp,kps->ksr', library[chosen], image_blocks[placed], preferr...  15 us
    dot_general x4, matrix products, adjoint_turn(): jnp.einsum('krp,ksr->kps', library[chosen], returned[sourced], preferred_...  10.4 us
    gather x4, local copies, waits for them, and re-layouts, forward_turn(): image_blocks[placed]  8.67 us
    gather x4, local copies, waits for them, and re-layouts, adjoint_turn(): library[chosen]  8.66 us
    gather x4, local copies, waits for them, and re-layouts, forward_turn(): library[chosen]  8.43 us
  transfers between devices with their start and end apart: 9, of which 5 were waited for; matrix products, arithmetic and copies ran while one was open for 33% of the time, Pallas kernels for 0%

profile of v1, /device:TPU:0, one launch (start us, length us, event | category | flops | bytes accessed | tf_op | source)
XLA Modules:
  0.0 200.4 jit_solution(6283780144326259690)
XLA Ops:
  8.0 2.4 %collective-permute-start = (bf16[1,64,64]{2,1,0:T(8,128)(2,1)S(1)}, bf16[1,64,64]{2,1,0:T(8,128)(2,1)S(1)}, u32[]{:S(2)}, u32[]{:S(2)}) collective-permute-start(bf16[1,64,64]{2,1,0:T(8,128)(2,1)S(1)} %get-tuple-element.333), channel_id=1, source_target_pairs={{0,1},{1,2},{2,3},{4,5},{5,6},{6,7},{8,9},{9,10},{10,11},{12,13},{... | collective-permute-start | bytes 24584 | tf_op jit(solution)/shard_map/ppermute | solution.py:18
  21.2 6.4 %all-to-all-start = ((bf16[8,2,8192]{2,1,0:T(2,128)(2,1)}), bf16[8,2,8192]{2,1,0:T(2,128)(2,1)}, u32[]{:S(2)}, u32[]{:S(2)}) async-start(bf16[8,2,8192]{2,1,0:T(2,128)(2,1)} %reshape.293), calls=%async_computation | async-start | bytes 524288 | tf_op jit(solution)/shard_map/all_to_all | solution.py:82
  27.7 47.9 %while.28 = (s32[]{:T(128)}, f32[8,64,128]{2,1,0:T(8,128)S(1)}, s32[256]{0:T(256)S(1)}, s32[256]{0:T(256)S(1)}, bf16[16,128,64]{2,1,0:T(8,128)(2,1)S(1)}, /*inde...) while((s32[]{:T(128)}, f32[8,64,128]{2,1,0:T(8,128)S(1)}, ...), condition=%wide.region_4.5_spmd, body=%wide.region_2.4_spmd.sunk | while | flops 134744640 | bytes 17836972 | solution.py:118
  27.9 2.2 %gather_fusion = bf16[64,128,64]{2,1,0:T(8,128)(2,1)} fusion(bf16[16,128,64]{2,1,0:T(8,128)(2,1)S(1)} %get-tuple-element.456, s32[1024]{0:T(1024)S(1)} %pad_clamp_fusion.8), kind=kCustom, calls=%fused_computation.clone.1 | custom fusion | bytes 2097408 | tf_op jit(solution)/shard_map/while/body/eval_jaxpr/gather | solution.py:113
  32.2 3.7 %fusion.79 = f32[64,64,128]{2,1,0:T(8,128)S(1)} fusion(bf16[64,128,64]{2,1,0:T(8,128)(2,1)} %gather_fusion, bf16[64,128,128]{2,1,0:T(8,128)(2,1)} %gather_fusion.1), kind=kOutput, calls=%fused_computation.129.clone.1 | convolution fusion | flops 134217728 | bytes 5242880 | tf_op jit(solution)/shard_map/while/body/eval_jaxpr/krp,kps->ksr/dot_general | solution.py:110
  35.9 3.8 %scatter_fusion = f32[8,64,128]{2,1,0:T(8,128)S(1)} fusion(f32[8,64,128]{2,1,0:T(8,128)S(1)} %get-tuple-element.442, s32[64]{0:T(128)S(1)} %compare_select_fusion.10, f32[64,64,128]{2,1,0:T(8,128)S(1)} %fusion.79), kind=kCustom, calls=%fused_computation.4.clone.1 | custom fusion | flops 524288 | bytes 6291712 | tf_op jit(solution)/shard_map/while/body/eval_jaxpr/scatter-add | solution.py:116
  39.9 2.2 %gather_fusion = bf16[64,128,64]{2,1,0:T(8,128)(2,1)} fusion(bf16[16,128,64]{2,1,0:T(8,128)(2,1)S(1)} %get-tuple-element.456, s32[1024]{0:T(1024)S(1)} %pad_clamp_fusion.8), kind=kCustom, calls=%fused_computation.clone.1 | custom fusion | bytes 2097408 | tf_op jit(solution)/shard_map/while/body/eval_jaxpr/gather | solution.py:113
  44.1 3.7 %fusion.79 = f32[64,64,128]{2,1,0:T(8,128)S(1)} fusion(bf16[64,128,64]{2,1,0:T(8,128)(2,1)} %gather_fusion, bf16[64,128,128]{2,1,0:T(8,128)(2,1)} %gather_fusion.1), kind=kOutput, calls=%fused_computation.129.clone.1 | convolution fusion | flops 134217728 | bytes 5242880 | tf_op jit(solution)/shard_map/while/body/eval_jaxpr/krp,kps->ksr/dot_general | solution.py:110
  47.9 3.8 %scatter_fusion = f32[8,64,128]{2,1,0:T(8,128)S(1)} fusion(f32[8,64,128]{2,1,0:T(8,128)S(1)} %get-tuple-element.442, s32[64]{0:T(128)S(1)} %compare_select_fusion.10, f32[64,64,128]{2,1,0:T(8,128)S(1)} %fusion.79), kind=kCustom, calls=%fused_computation.4.clone.1 | custom fusion | flops 524288 | bytes 6291712 | tf_op jit(solution)/shard_map/while/body/eval_jaxpr/scatter-add | solution.py:116
  51.8 2.2 %gather_fusion = bf16[64,128,64]{2,1,0:T(8,128)(2,1)} fusion(bf16[16,128,64]{2,1,0:T(8,128)(2,1)S(1)} %get-tuple-element.456, s32[1024]{0:T(1024)S(1)} %pad_clamp_fusion.8), kind=kCustom, calls=%fused_computation.clone.1 | custom fusion | bytes 2097408 | tf_op jit(solution)/shard_map/while/body/eval_jaxpr/gather | solution.py:113
  56.1 3.7 %fusion.79 = f32[64,64,128]{2,1,0:T(8,128)S(1)} fusion(bf16[64,128,64]{2,1,0:T(8,128)(2,1)} %gather_fusion, bf16[64,128,128]{2,1,0:T(8,128)(2,1)} %gather_fusion.1), kind=kOutput, calls=%fused_computation.129.clone.1 | convolution fusion | flops 134217728 | bytes 5242880 | tf_op jit(solution)/shard_map/while/body/eval_jaxpr/krp,kps->ksr/dot_general | solution.py:110
  59.9 3.8 %scatter_fusion = f32[8,64,128]{2,1,0:T(8,128)S(1)} fusion(f32[8,64,128]{2,1,0:T(8,128)S(1)} %get-tuple-element.442, s32[64]{0:T(128)S(1)} %compare_select_fusion.10, f32[64,64,128]{2,1,0:T(8,128)S(1)} %fusion.79), kind=kCustom, calls=%fused_computation.4.clone.1 | custom fusion | flops 524288 | bytes 6291712 | tf_op jit(solution)/shard_map/while/body/eval_jaxpr/scatter-add | solution.py:116
  63.8 2.2 %gather_fusion = bf16[64,128,64]{2,1,0:T(8,128)(2,1)} fusion(bf16[16,128,64]{2,1,0:T(8,128)(2,1)S(1)} %get-tuple-element.456, s32[1024]{0:T(1024)S(1)} %pad_clamp_fusion.8), kind=kCustom, calls=%fused_computation.clone.1 | custom fusion | bytes 2097408 | tf_op jit(solution)/shard_map/while/body/eval_jaxpr/gather | solution.py:113
  68.1 3.7 %fusion.79 = f32[64,64,128]{2,1,0:T(8,128)S(1)} fusion(bf16[64,128,64]{2,1,0:T(8,128)(2,1)} %gather_fusion, bf16[64,128,128]{2,1,0:T(8,128)(2,1)} %gather_fusion.1), kind=kOutput, calls=%fused_computation.129.clone.1 | convolution fusion | flops 134217728 | bytes 5242880 | tf_op jit(solution)/shard_map/while/body/eval_jaxpr/krp,kps->ksr/dot_general | solution.py:110
  71.8 3.8 %scatter_fusion = f32[8,64,128]{2,1,0:T(8,128)S(1)} fusion(f32[8,64,128]{2,1,0:T(8,128)S(1)} %get-tuple-element.442, s32[64]{0:T(128)S(1)} %compare_select_fusion.10, f32[64,64,128]{2,1,0:T(8,128)S(1)} %fusion.79), kind=kCustom, calls=%fused_computation.4.clone.1 | custom fusion | flops 524288 | bytes 6291712 | tf_op jit(solution)/shard_map/while/body/eval_jaxpr/scatter-add | solution.py:116
  76.3 6.0 %all-to-all-start.2 = ((bf16[8,64,128]{2,1,0:T(8,128)(2,1)}), bf16[8,64,128]{2,1,0:T(8,128)(2,1)S(1)}, u32[]{:S(2)}, u32[]{:S(2)}) async-start(bf16[8,64,128]{2,1,0:T(8,128)(2,1)} %convert_element_type.108), calls=%async_computation.2 | async-start | bytes 262144 | tf_op jit(solution)/shard_map/all_to_all | solution.py:121
  84.2 4.8 %sort.16 = (f32[8,8,2048]{2,0,1:T(8,128)S(1)}, s32[8,8,2048]{2,0,1:T(8,128)}) sort(f32[8,8,2048]{2,0,1:T(8,128)S(1)} %copy_select_fusion, s32[8,8,2048]{2,0,1:T(8,128)S(1)} %iota.19), dimensions={0}, to_apply=%region_1.2 | sort | flops 2228224 | bytes 2097152 | tf_op jit(solution)/shard_map/jit(median)/jit(quantile)/sort | solution.py:54
  90.5 4.1 %collective-permute-start.2 = (f32[8,8]{1,0:T(8,128)S(1)}, f32[8,8]{1,0:T(8,128)S(1)}, u32[]{:S(2)}, u32[]{:S(2)}) collective-permute-start(f32[8,8]{1,0:T(8,128)S(1)} %get-tuple-element.334), channel_id=1, source_target_pairs={{0,1},{1,2},{2,3},{4,5},{5,6},{6,7},{8,9},{9,10},{10,11},{12,13},{... | collective-permute-start | bytes 776 | tf_op jit(solution)/shard_map/ppermute | solution.py:18
  100.9 5.7 %all-to-all-start.1 = ((bf16[8,1,8,2048]{3,2,1,0:T(8,128)(2,1)}), bf16[8,1,8,2048]{3,2,1,0:T(8,128)(2,1)S(1)}, u32[]{:S(2)}, u32[]{:S(2)}) async-start(bf16[8,1,8,2048]{3,2,1,0:T(8,128)(2,1)} %fusion.42), calls=%async_computation.1 | async-start | bytes 524288 | tf_op jit(solution)/shard_map/all_to_all | solution.py:88
  106.9 8.1 %all-to-all-done.1 = bf16[8,1,8,2048]{3,2,1,0:T(8,128)(2,1)S(1)} async-done(((bf16[8,1,8,2048]{3,2,1,0:T(8,128)(2,1)}), bf16[8,1,8,2048]{3,2,1,0:T(8,128)(2,1)S(1)}, u32[]{:S(2)}, u32[]{:S(2)}) %all-to-all-start.1) | async-done | bytes 262176 | tf_op jit(solution)/shard_map/all_to_all | solution.py:88
  116.1 5.0 %all-to-all-start.3 = ((bf16[8,64,128]{2,1,0:T(8,128)(2,1)}), bf16[8,64,128]{2,1,0:T(8,128)(2,1)S(1)}, u32[]{:S(2)}, u32[]{:S(2)}) async-start(bf16[8,64,128]{2,1,0:T(8,128)(2,1)} %copy.47), calls=%async_computation.3 | async-start | bytes 262144 | tf_op jit(solution)/shard_map/all_to_all | solution.py:138
  121.1 7.4 %all-to-all-done.3 = bf16[8,64,128]{2,1,0:T(8,128)(2,1)S(1)} async-done(((bf16[8,64,128]{2,1,0:T(8,128)(2,1)}), bf16[8,64,128]{2,1,0:T(8,128)(2,1)S(1)}, u32[]{:S(2)}, u32[]{:S(2)}) %all-to-all-start.3) | async-done | bytes 131104 | tf_op jit(solution)/shard_map/all_to_all | solution.py:138
  128.6 41.5 %while.29 = (s32[]{:T(128)}, f32[16,128,64]{1,2,0:T(8,128)S(1)}, s32[256]{0:T(256)S(1)}, s32[256]{0:T(256)S(1)}, bf16[16,128,128]{2,1,0:T(8,128)(2,1)S(1)}, /*in...) while((s32[]{:T(128)}, f32[16,128,64]{1,2,0:T(8,128)S(1)}, ...), condition=%wide.region_7.8_spmd, body=%wide.region_5.7_spmd.sunk | while | flops 134744640 | bytes 17836972 | solution.py:150
  132.6 2.6 %fusion.82 = f32[64,128,64]{1,2,0:T(8,128)S(1)} fusion(bf16[64,64,128]{2,1,0:T(8,128)(2,1)} %gather_fusion.2, bf16[64,128,128]{2,1,0:T(8,128)(2,1)} %gather_fusion.3), kind=kOutput, calls=%fused_computation.130.clone.1 | convolution fusion | flops 134217728 | bytes 5242880 | tf_op jit(solution)/shard_map/while/body/eval_jaxpr/krp,ksr->kps/dot_general | solution.py:145
  135.2 3.7 %scatter_fusion.1 = f32[16,128,64]{1,2,0:T(8,128)S(1)} fusion(f32[16,128,64]{1,2,0:T(8,128)S(1)} %get-tuple-element.475, s32[64]{0:T(128)S(1)} %compare_select_fusion.12, f32[64,128,64]{1,2,0:T(8,128)S(1)} %fusion.82), kind=kCustom, calls=%fused_computation.5.clone.1 | custom fusion | flops 524288 | bytes 6291712 | tf_op jit(solution)/shard_map/while/body/eval_jaxpr/scatter-add | solution.py:148
  143.0 2.6 %fusion.82 = f32[64,128,64]{1,2,0:T(8,128)S(1)} fusion(bf16[64,64,128]{2,1,0:T(8,128)(2,1)} %gather_fusion.2, bf16[64,128,128]{2,1,0:T(8,128)(2,1)} %gather_fusion.3), kind=kOutput, calls=%fused_computation.130.clone.1 | convolution fusion | flops 134217728 | bytes 5242880 | tf_op jit(solution)/shard_map/while/body/eval_jaxpr/krp,ksr->kps/dot_general | solution.py:145
  145.5 3.8 %scatter_fusion.1 = f32[16,128,64]{1,2,0:T(8,128)S(1)} fusion(f32[16,128,64]{1,2,0:T(8,128)S(1)} %get-tuple-element.475, s32[64]{0:T(128)S(1)} %compare_select_fusion.12, f32[64,128,64]{1,2,0:T(8,128)S(1)} %fusion.82), kind=kCustom, calls=%fused_computation.5.clone.1 | custom fusion | flops 524288 | bytes 6291712 | tf_op jit(solution)/shard_map/while/body/eval_jaxpr/scatter-add | solution.py:148
  153.3 2.6 %fusion.82 = f32[64,128,64]{1,2,0:T(8,128)S(1)} fusion(bf16[64,64,128]{2,1,0:T(8,128)(2,1)} %gather_fusion.2, bf16[64,128,128]{2,1,0:T(8,128)(2,1)} %gather_fusion.3), kind=kOutput, calls=%fused_computation.130.clone.1 | convolution fusion | flops 134217728 | bytes 5242880 | tf_op jit(solution)/shard_map/while/body/eval_jaxpr/krp,ksr->kps/dot_general | solution.py:145
  155.9 3.8 %scatter_fusion.1 = f32[16,128,64]{1,2,0:T(8,128)S(1)} fusion(f32[16,128,64]{1,2,0:T(8,128)S(1)} %get-tuple-element.475, s32[64]{0:T(128)S(1)} %compare_select_fusion.12, f32[64,128,64]{1,2,0:T(8,128)S(1)} %fusion.82), kind=kCustom, calls=%fused_computation.5.clone.1 | custom fusion | flops 524288 | bytes 6291712 | tf_op jit(solution)/shard_map/while/body/eval_jaxpr/scatter-add | solution.py:148
  163.7 2.6 %fusion.82 = f32[64,128,64]{1,2,0:T(8,128)S(1)} fusion(bf16[64,64,128]{2,1,0:T(8,128)(2,1)} %gather_fusion.2, bf16[64,128,128]{2,1,0:T(8,128)(2,1)} %gather_fusion.3), kind=kOutput, calls=%fused_computation.130.clone.1 | convolution fusion | flops 134217728 | bytes 5242880 | tf_op jit(solution)/shard_map/while/body/eval_jaxpr/krp,ksr->kps/dot_general | solution.py:145
  166.3 3.8 %scatter_fusion.1 = f32[16,128,64]{1,2,0:T(8,128)S(1)} fusion(f32[16,128,64]{1,2,0:T(8,128)S(1)} %get-tuple-element.475, s32[64]{0:T(128)S(1)} %compare_select_fusion.12, f32[64,128,64]{1,2,0:T(8,128)S(1)} %fusion.82), kind=kCustom, calls=%fused_computation.5.clone.1 | custom fusion | flops 524288 | bytes 6291712 | tf_op jit(solution)/shard_map/while/body/eval_jaxpr/scatter-add | solution.py:148
  172.8 19.1 %reduce-scatter.2.cloned.1.call-done = f32[512,64]{0,1:T(8,128)} async-done(((f32[2048,64]{0,1:T(8,128)}), f32[512,64]{0,1:T(8,128)}) %reduce-scatter.2.cloned.1.call-update) | async-done | bytes 131088 | tf_op jit(solution)/shard_map/reduce_scatter | solution.py:155
  (115 shorter events, 52.1 us)
Async XLA Ops:
  8.0 7.3 %collective-permute-start = (bf16[1,64,64]{2,1,0:T(8,128)(2,1)S(1)}, bf16[1,64,64]{2,1,0:T(8,128)(2,1)S(1)}, u32[]{:S(2)}, u32[]{:S(2)}) collective-permute-start(bf16[1,64,64]{2,1,0:T(8,128)(2,1)S(1)} %get-tuple-element.333), channel_id=1, source_target_pairs={{0,1},{1,2},{2,3},{4,5},{5,6},{6,7},{8,9},{9,10},{10,11},{12,13},{... | collective-permute-start | bytes 24584 | tf_op jit(solution)/shard_map/ppermute | solution.py:18
  10.4 5.2 %collective-permute-start.1 = (bf16[1,64,64]{2,1,0:T(8,128)(2,1)S(1)}, bf16[1,64,64]{2,1,0:T(8,128)(2,1)S(1)}, u32[]{:S(2)}, u32[]{:S(2)}) collective-permute-start(bf16[1,64,64]{2,1,0:T(8,128)(2,1)S(1)} %get-tuple-element.332), channel_id=1, source_target_pairs={{1,0},{2,1},{3,2},{5,4},{6,5},{7,6},{9,8},{10,9},{11,10},{13,12},{... | collective-permute-start | bytes 24584 | tf_op jit(solution)/shard_map/ppermute | solution.py:20
  17.1 10.6 %copy-start = (bf16[1,1,16,128,128]{4,3,2,1,0:T(8,128)(2,1)S(1)}, bf16[1,1,16,128,128]{4,3,2,1,0:T(8,128)(2,1)}, u32[]{:S(2)}) copy-start(bf16[1,1,16,128,128]{4,3,2,1,0:T(8,128)(2,1)} %param.16) | copy-start | bytes 1572868
  17.1 10.6 %copy-start.2 = (s32[1,1,256]{2,1,0:T(1,128)S(1)}, s32[1,1,256]{2,1,0:T(1,128)}, u32[]{:S(2)}) copy-start(s32[1,1,256]{2,1,0:T(1,128)} %param.17) | copy-start | bytes 3076
  17.1 10.6 %copy-start.3 = (s32[1,1,256]{2,1,0:T(1,128)S(1)}, s32[1,1,256]{2,1,0:T(1,128)}, u32[]{:S(2)}) copy-start(s32[1,1,256]{2,1,0:T(1,128)} %param.18) | copy-start | bytes 3076
  21.2 55.1 %all-to-all-start = ((bf16[8,2,8192]{2,1,0:T(2,128)(2,1)}), bf16[8,2,8192]{2,1,0:T(2,128)(2,1)}, u32[]{:S(2)}, u32[]{:S(2)}) async-start(bf16[8,2,8192]{2,1,0:T(2,128)(2,1)} %reshape.293), calls=%async_computation | async-start | bytes 524288 | tf_op jit(solution)/shard_map/all_to_all | solution.py:82
  76.3 24.6 %all-to-all-start.2 = ((bf16[8,64,128]{2,1,0:T(8,128)(2,1)}), bf16[8,64,128]{2,1,0:T(8,128)(2,1)S(1)}, u32[]{:S(2)}, u32[]{:S(2)}) async-start(bf16[8,64,128]{2,1,0:T(8,128)(2,1)} %convert_element_type.108), calls=%async_computation.2 | async-start | bytes 262144 | tf_op jit(solution)/shard_map/all_to_all | solution.py:121
  84.2 22.4 %copy-start.5 = (s32[1,1,8]{2,1,0:T(1,128)S(1)}, s32[1,1,8]{2,1,0:T(1,128)}, u32[]{:S(2)}) copy-start(s32[1,1,8]{2,1,0:T(1,128)} %param.21) | copy-start | bytes 100
  89.2 5.4 %collective-permute-start.3 = (f32[8,8]{1,0:T(8,128)S(1)}, f32[8,8]{1,0:T(8,128)S(1)}, u32[]{:S(2)}, u32[]{:S(2)}) collective-permute-start(f32[8,8]{1,0:T(8,128)S(1)} %get-tuple-element.335), channel_id=1, source_target_pairs={{1,0},{2,1},{3,2},{5,4},{6,5},{7,6},{9,8},{10,9},{11,10},{13,12},{... | collective-permute-start | bytes 776 | tf_op jit(solution)/shard_map/ppermute | solution.py:20
  90.5 4.9 %collective-permute-start.2 = (f32[8,8]{1,0:T(8,128)S(1)}, f32[8,8]{1,0:T(8,128)S(1)}, u32[]{:S(2)}, u32[]{:S(2)}) collective-permute-start(f32[8,8]{1,0:T(8,128)S(1)} %get-tuple-element.334), channel_id=1, source_target_pairs={{0,1},{1,2},{2,3},{4,5},{5,6},{6,7},{8,9},{9,10},{10,11},{12,13},{... | collective-permute-start | bytes 776 | tf_op jit(solution)/shard_map/ppermute | solution.py:18
  100.9 14.2 %all-to-all-start.1 = ((bf16[8,1,8,2048]{3,2,1,0:T(8,128)(2,1)}), bf16[8,1,8,2048]{3,2,1,0:T(8,128)(2,1)S(1)}, u32[]{:S(2)}, u32[]{:S(2)}) async-start(bf16[8,1,8,2048]{3,2,1,0:T(8,128)(2,1)} %fusion.42), calls=%async_computation.1 | async-start | bytes 524288 | tf_op jit(solution)/shard_map/all_to_all | solution.py:88
  106.9 9.2 %copy-start.1 = (f32[1,64,16,128]{3,2,1,0:T(8,128)}, f32[1,64,16,128]{3,2,1,0:T(8,128)S(1)}, u32[]{:S(2)}) copy-start(f32[1,64,16,128]{3,2,1,0:T(8,128)S(1)} %convolution_bitcast_fusion) | copy-start | bytes 1572868
  106.9 21.7 %copy-start.4 = (s32[1,1,256]{2,1,0:T(1,128)S(1)}, s32[1,1,256]{2,1,0:T(1,128)}, u32[]{:S(2)}) copy-start(s32[1,1,256]{2,1,0:T(1,128)} %param.19) | copy-start | bytes 3076
  116.1 12.5 %all-to-all-start.3 = ((bf16[8,64,128]{2,1,0:T(8,128)(2,1)}), bf16[8,64,128]{2,1,0:T(8,128)(2,1)S(1)}, u32[]{:S(2)}, u32[]{:S(2)}) async-start(bf16[8,64,128]{2,1,0:T(8,128)(2,1)} %copy.47), calls=%async_computation.3 | async-start | bytes 262144 | tf_op jit(solution)/shard_map/all_to_all | solution.py:138
  121.1 70.9 %reduce-scatter.2.cloned.1.call-start = ((), (), s32[]{:S(2)}) async-start(), calls=%async_computation.5 | async-start | bytes 655360 | tf_op jit(solution)/shard_map/reduce_scatter | solution.py:155
Sparse Core Ops, SparseCore 0:
  171.1 20.8 reduce-scatter.1
